TPU v7x, 8 devices: a whole 2x2x1 slice. The times are simulated.
8 devices in a mesh: dp: 2 (over z, y), ep: 4 (over x, core).
Axes of the slice: x: 2, y: 2, z: 1, core: 2. Of those that a mesh axis runs over, the one named last changes fastest.
Arguments:
- hidden: bfloat16 [8192, 2048], P(('dp', 'ep')), parts along dimension 0
- expert_ids: int32 [8192, 2], P(('dp', 'ep')), parts along dimension 0
- norm_gain: bfloat16 [2048], replicated
- w_router: bfloat16 [2048, 8], replicated
- w_gate: bfloat16 [8, 2048, 5632], P('ep')
- w_up: bfloat16 [8, 2048, 5632], P('ep')
- w_down: bfloat16 [8, 5632, 2048], P('ep')
Outputs:
- output: bfloat16 [8192, 2048], P(('dp', 'ep')), parts along dimension 0
There are 2 independent parts. A program takes and returns all parts, laid end to end along the dimension named above; an argument that names none is the same for every part.
All inputs are finite; a program needn't handle non-finite values.
Results may differ from a plain program's by a relative error of at most 0.00119.
Values are sent between devices in bfloat16 or wider.
A program may use at most 1 GiB of HBM per device.

v0:
```python
import functools

import jax
import jax.numpy as jnp
from jax import lax
from jax.experimental import pallas as pl
from jax.experimental.pallas import tpu as pltpu
from jax.sharding import PartitionSpec as P


NORM_EPS = 1e-5
F32 = jnp.float32
BF16 = jnp.bfloat16
BLK = 16
TAIL = 48
NBUF = 3
TF = 512
ANY = pl.BlockSpec(memory_space=pl.ANY)
SMEM = pl.BlockSpec(memory_space=pltpu.SMEM)
VMEM = pl.BlockSpec(memory_space=pltpu.VMEM)
HBM = pl.BlockSpec(memory_space=pltpu.HBM)
MIB = 2**20


def up_to(n, m):
    return (n + m - 1) // m * m


def peers_of(group):
    me = lax.axis_index("ep")
    return [me, me + 1 - 2 * lax.rem(me, 2), lax.rem(me + 2, group), group - 1 - me]


def pack_rows(normed, queue, wanted, lo, count):
    rows = lo + lax.broadcasted_iota(jnp.int32, (count, queue.shape[1]), 0)
    hit, shift = None, None
    for expert in wanted:
        place = queue[pl.ds(expert, 1), :]
        kept = place >= 0
        at = place if shift is None else jnp.where(kept, place + shift, -1)
        here = rows == at
        hit = here if hit is None else hit | here
        held = jnp.sum(kept.astype(F32), axis=1, keepdims=True).astype(jnp.int32)
        shift = (held + (BLK - 1)) // BLK * BLK
    return jnp.dot(hit.astype(F32).astype(BF16), normed, preferred_element_type=F32).astype(BF16)


def emit_packs(cap, normed, queue, jobs, outs, slots, sem):
    copies = []
    outs = list(outs)
    for k, (wanted, lo) in enumerate(jobs):
        slots[k] = pack_rows(normed[...], queue, wanted, lo, cap)
        at = 0
        while at < cap:
            out = outs.pop(0)
            copies.append(pltpu.make_async_copy(slots.at[k, pl.ds(at, out.shape[0])], out, sem.at[len(copies)]))
            copies[-1].start()
            at += out.shape[0]
    for copy in copies:
        copy.wait()


def route_kernel(group, per, cap, hid_hbm, idst, gain, w_router_t, normed_hbm, queue, meta, table, *rest):
    far0, (hid, normed, row_sem, slots, sem, mine, held, send_sem, recv_sem) = rest[:2], rest[2:]
    tok = hid.shape[0]
    step = 256
    loads = [pltpu.make_async_copy(hid_hbm.at[pl.ds(i, step)], hid.at[pl.ds(i, step)], row_sem.at[i // step])
             for i in range(0, tok, step)]
    for copy in loads:
        copy.start()
    peers = peers_of(group)
    other = 1 - lax.axis_index("dp")
    mates = [{"ep": peer} for peer in peers[1:]] + [{"dp": other, "ep": peer} for peer in peers]
    barrier = pltpu.get_barrier_semaphore()
    for mate in mates:
        pl.semaphore_signal(barrier, inc=1, device_id=mate, device_id_type=pl.DeviceIdType.MESH)

    experts = w_router_t.shape[0]
    eye = lax.broadcasted_iota(jnp.int32, (experts, tok), 0)
    hit0 = (idst[0:1, :] == eye).astype(F32)
    hit1 = (idst[1:2, :] == eye).astype(F32)
    both = jnp.concatenate([hit0, hit1], axis=0).astype(BF16)
    total = lax.dot_general(jnp.ones((8, tok), BF16), (hit0 + hit1).astype(BF16), (((1,), (1,)), ((), ())),
                            preferred_element_type=F32)
    mine[...] = jnp.zeros_like(mine)
    mine[:, 0:experts] = jnp.minimum(total, float(cap)).astype(jnp.int32)

    for i in range(0, tok, step):
        loads[i // step].wait()
        x = hid[i:i + step, :].astype(F32)
        mean_sq = jnp.mean(x * x, axis=-1, keepdims=True)
        normed[i:i + step, :] = (x * lax.rsqrt(mean_sq + NORM_EPS) * gain[...].astype(F32).reshape(1, -1)).astype(BF16)

    keep = pltpu.make_async_copy(normed, normed_hbm, row_sem.at[tok // step])
    keep.start()
    pl.semaphore_wait(barrier, len(mates))
    sends = [pltpu.make_async_remote_copy(
        src_ref=mine, dst_ref=held.at[k], send_sem=send_sem.at[k], recv_sem=recv_sem.at[k],
        device_id=mate, device_id_type=pl.DeviceIdType.MESH) for k, mate in enumerate(mates)]
    for copy in sends:
        copy.start()

    logits = lax.dot_general(w_router_t[...], normed[...], (((1,), (1,)), ((), ())), preferred_element_type=F32)
    tot0 = jnp.sum(hit0, axis=1, keepdims=True)
    parts = []
    for i in range(0, tok, step):
        before = (lax.broadcasted_iota(jnp.int32, (tok, step), 0)
                  < i + lax.broadcasted_iota(jnp.int32, (tok, step), 1)).astype(F32).astype(BF16)
        parts.append(jnp.dot(both, before, preferred_element_type=F32))
    seen = jnp.concatenate(parts, axis=1)
    place = jnp.where(hit0 > 0, seen[:experts], jnp.where(hit1 > 0, seen[experts:] + tot0, -1.0))
    queue[...] = jnp.where(place < float(cap), place, -1.0).astype(jnp.int32)

    code = jnp.where(place < float(cap), eye.astype(F32) * float(cap) + place, -1.0)
    l0 = jnp.sum(hit0 * logits, axis=0, keepdims=True)
    l1 = jnp.sum(hit1 * logits, axis=0, keepdims=True)
    top = jnp.maximum(l0, l1)
    e0, e1 = jnp.exp(l0 - top), jnp.exp(l1 - top)
    lines = jnp.concatenate([jnp.sum(hit0 * code, axis=0, keepdims=True), jnp.sum(hit1 * code, axis=0, keepdims=True),
                             e0 / (e0 + e1), e1 / (e0 + e1), jnp.zeros((4, tok), F32)], axis=0)
    meta[...] = lines.T
    emit_packs(cap, normed, queue, [([per * peers[k], per * peers[k] + 1], 0) for k in (2, 3)], far0, slots, sem)

    keep.wait()
    table[...] = jnp.zeros_like(table)
    table[0:1, :] = mine[0:1, :]
    for k, copy in enumerate(sends):
        copy.wait()
        table[k + 1:k + 2, :] = held[k, 0:1, :]


def route(hidden, idst, gain, w_router_t, group, cap):
    tok, width = hidden.shape
    experts = w_router_t.shape[0]
    one = jax.ShapeDtypeStruct((cap, width), BF16)
    return pl.pallas_call(
        functools.partial(route_kernel, group, experts // group, cap),
        out_shape=[jax.ShapeDtypeStruct((tok, width), BF16), jax.ShapeDtypeStruct((experts, tok), jnp.int32),
                   jax.ShapeDtypeStruct((tok, 8), F32), jax.ShapeDtypeStruct((8, 128), jnp.int32), one, one],
        in_specs=[HBM] + [VMEM] * 3,
        out_specs=[HBM] + [VMEM] * 3 + [HBM] * 2,
        scratch_shapes=[pltpu.VMEM((tok, width), BF16), pltpu.VMEM((tok, width), BF16), pltpu.SemaphoreType.DMA((5,)),
                        pltpu.VMEM((2, cap, width), BF16), pltpu.SemaphoreType.DMA((2,)),
                        pltpu.VMEM((8, 128), jnp.int32), pltpu.VMEM((2 * group - 1, 8, 128), jnp.int32),
                        pltpu.SemaphoreType.DMA((2 * group - 1,)), pltpu.SemaphoreType.DMA((2 * group - 1,))],
        cost_estimate=pl.CostEstimate(flops=10**10, bytes_accessed=2 * 10**7, transcendentals=0),
        compiler_params=pltpu.CompilerParams(collective_id=0, has_side_effects=True, vmem_limit_bytes=62 * MIB),
    )(hidden, idst, gain, w_router_t)


def pack_kernel(group, per, cap, jobs, n_out, normed, queue, *rest):
    outs, (slots, sem) = rest[:n_out], rest[n_out:]
    peers = peers_of(group)
    emit_packs(cap, normed, queue, [([per * peers[k] + i for i in which], lo) for k, which, lo in jobs], outs, slots, sem)


def pack(jobs, sizes, normed, queue, group, cap):
    _, width = normed.shape
    n = len(sizes)
    return pl.pallas_call(
        functools.partial(pack_kernel, group, queue.shape[0] // group, cap, jobs, n),
        out_shape=[jax.ShapeDtypeStruct((size, width), BF16) for size in sizes],
        in_specs=[VMEM] * 2,
        out_specs=[HBM] * n,
        scratch_shapes=[pltpu.VMEM((len(jobs), cap, width), BF16), pltpu.SemaphoreType.DMA((n,))],
        cost_estimate=pl.CostEstimate(flops=9 * 10**9, bytes_accessed=2 * 10**7, transcendentals=0),
        compiler_params=pltpu.CompilerParams(vmem_limit_bytes=62 * MIB),
    )(normed, queue)


def move_rows(src, at, dst, to, count):
    def one(c, _):
        dst[pl.ds(pl.multiple_of(to + c * BLK, BLK), BLK), :] = src[pl.ds(pl.multiple_of(at + c * BLK, BLK), BLK), :]
        return 0

    lax.fori_loop(0, count // BLK, one, 0)


def ffn_kernel(mode, local, per, dist, cap, sizes, n_in, n_out, table, *refs):
    ins, (wg, wu, wd), refs = refs[:n_in], refs[n_in:n_in + 3], refs[n_in + 3:]
    outs, (xs, acc, bg, bu, bd, wsem, sem, *more) = refs[:n_out], refs[n_out:]
    steps = wg.shape[2] // TF
    expert = per * lax.axis_index("ep") + local
    n0 = pl.multiple_of((table[dist, expert] + BLK - 1) // BLK * BLK, BLK)
    rows = n0 + table[dist + 1, expert]

    def copies(f, slot):
        cols = pl.ds(pl.multiple_of(f * TF, TF), TF)
        return (pltpu.make_async_copy(wg.at[local, :, cols], bg.at[slot], wsem.at[0, slot]),
                pltpu.make_async_copy(wu.at[local, :, cols], bu.at[slot], wsem.at[1, slot]),
                pltpu.make_async_copy(wd.at[local, cols, :], bd.at[slot], wsem.at[2, slot]))

    def fetch(f, slot):
        for c in copies(f, slot):
            c.start()

    def start(copies):
        for c in copies:
            c.start()

    def wait(copies):
        for c in copies:
            c.wait()

    if mode == "far1":
        packed, tails = more
        first = [table[dist + k, expert - 1] for k in range(2)]
        loads = []
        for k in range(2):
            at = 0
            for x in ins[k:6:2]:
                loads.append(pltpu.make_async_copy(x, packed.at[k, pl.ds(at, x.shape[0])], sem.at[len(loads)]))
                at += x.shape[0]
            loads.append(pltpu.make_async_copy(ins[6 + k], tails.at[k], sem.at[len(loads)]))
        start(loads)
        fetch(0, 0)
        acc[...] = jnp.zeros_like(acc)
        wait(loads)
        for k, to in enumerate((0, n0)):
            move_rows(packed.at[k], (first[k] + BLK - 1) // BLK * BLK, xs, to, cap)
    else:
        load = [pltpu.make_async_copy(x.at[pl.ds(0, cap)], xs.at[pl.ds(to, cap)], sem.at[k])
                for k, (x, to) in enumerate(zip(ins, (0, n0)))]
        load[0].start()
        fetch(0, 0)
        load[0].wait()
        load[1].start()
        acc[...] = jnp.zeros_like(acc)
        load[1].wait()

    def step(f, _):
        slot = lax.rem(f, NBUF)
        for c in copies(f, slot):
            c.wait()

        @pl.when(f == 0)
        def _():
            for k in range(1, NBUF - 1):
                fetch(k, k)

        @pl.when(f + NBUF - 1 < steps)
        def _():
            fetch(f + NBUF - 1, lax.rem(f + NBUF - 1, NBUF))

        def tile(m):
            x = xs[0:m, :]
            g = jnp.dot(x, bg[slot], preferred_element_type=F32)
            u = jnp.dot(x, bu[slot], preferred_element_type=F32)
            a = (jax.nn.silu(g) * u).astype(BF16)
            acc[0:m, :] += jnp.dot(a, bd[slot], preferred_element_type=F32)

        low = 0
        for m in sizes:
            @pl.when((rows > low) & (rows <= m))
            def _():
                tile(m)

            low = m
        return 0

    lax.fori_loop(0, steps, step, 0)
    xs[...] = acc[...].astype(BF16)
    stores = []
    for k, at in enumerate((0, n0)):
        source = xs
        if mode == "far1":
            source = packed.at[k]
            move_rows(xs, at, source, 0, cap)

            @pl.when(first[k] > cap - TAIL)
            def _():
                move_rows(tails.at[k], 0, source, (table[dist + k, expert] + BLK - 1) // BLK * BLK, TAIL)

            at = 0
        for out in outs[k::2]:
            stores.append(pltpu.make_async_copy(source.at[pl.ds(at, out.shape[0])], out, sem.at[len(stores)]))
            at += out.shape[0]
    start(stores)
    wait(stores)


def ffn(mode, table, xs, out_rows, wg, wu, wd, local, dist, cap):
    width, inner = wg.shape[1:]
    sizes = tuple(2 * cap - back for back in (192, 160, 128, 96, 64, 0))
    return pl.pallas_call(
        functools.partial(ffn_kernel, mode, local, wg.shape[0], dist, cap, sizes, len(xs), len(out_rows)),
        out_shape=[jax.ShapeDtypeStruct((rows, width), BF16) for rows in out_rows],
        in_specs=[SMEM] + [ANY] * (3 + len(xs)),
        out_specs=[HBM] * len(out_rows),
        scratch_shapes=[pltpu.VMEM((2 * cap, width), BF16), pltpu.VMEM((2 * cap, width), F32),
                        pltpu.VMEM((NBUF, width, TF), BF16), pltpu.VMEM((NBUF, width, TF), BF16),
                        pltpu.VMEM((NBUF, TF, width), BF16),
                        pltpu.SemaphoreType.DMA((3, NBUF)), pltpu.SemaphoreType.DMA((8,))]
        + ([pltpu.VMEM((2, 2 * cap, width), BF16), pltpu.VMEM((2, TAIL, width), BF16)] if mode == "far1" else []),
        cost_estimate=pl.CostEstimate(flops=6 * 540 * width * inner, bytes_accessed=6 * width * inner, transcendentals=0),
        compiler_params=pltpu.CompilerParams(vmem_limit_bytes=62 * MIB),
    )(table, *xs, wg, wu, wd)


def merge_kernel(group, per, cap, n_buf, far, table, meta, *refs):
    base, refs = refs[:2 * far], refs[2 * far:]
    bufs, (out, held, tgt, sem) = refs[:n_buf], refs[n_buf:]
    spots = [0]
    for buf in bufs:
        spots.append(spots[-1] + buf.shape[0])

    @pl.when(pl.program_id(0) == 0)
    def _():
        copies = [pltpu.make_async_copy(buf, held.at[pl.ds(spots[j], buf.shape[0])], sem.at[j])
                  for j, buf in enumerate(bufs)]
        for copy in copies:
            copy.start()
        peers = peers_of(group)
        lane = lax.broadcasted_iota(jnp.int32, tgt.shape, 1)
        want = jnp.full(tgt.shape, -2, jnp.int32)
        runs = []
        for k in range(2):
            if far:
                e0 = per * peers[2 + k]
                at = 2 * k * cap
                n1 = table[0, e0 + 1]
                runs.append((at, cap - TAIL, e0 * cap))
                runs.append((at + cap - TAIL, n1, (e0 + 1) * cap))
                runs.append((at + cap - TAIL + (n1 + BLK - 1) // BLK * BLK,
                             jnp.maximum(table[0, e0] - (cap - TAIL), 0), e0 * cap + cap - TAIL))
            else:
                runs += [((2 * k + i) * cap, cap, (per * peers[k] + i) * cap) for i in range(2)]
        for at, count, code in runs:
            want = jnp.where((lane >= at) & (lane < at + count), code + lane - at, want)
        tgt[...] = want.astype(F32)
        for copy in copies:
            copy.wait()

    rows = meta.shape[0]
    pick = jnp.concatenate([(meta[:, s:s + 1] == tgt[0:1, :]).astype(F32).astype(BF16) for s in range(2)], axis=0)
    got = jnp.dot(pick, held[...], preferred_element_type=F32)
    total = meta[:, 2:3] * got[:rows] + meta[:, 3:4] * got[rows:]
    if far:
        total = base[1][...].astype(F32) + (base[0][...] + total)
    out[...] = total.astype(out.dtype)


def merge(table, meta, bufs, group, per, cap, base=()):
    tok, width = meta.shape[0], bufs[0].shape[1]
    deep = 4 * cap
    rows = 256
    tile = pl.BlockSpec((rows, width), lambda i: (i, 0))
    return pl.pallas_call(
        functools.partial(merge_kernel, group, per, cap, len(bufs), len(base) > 0),
        out_shape=jax.ShapeDtypeStruct((tok, width), BF16 if base else F32),
        grid=(tok // rows,),
        in_specs=[SMEM, pl.BlockSpec((rows, 8), lambda i: (i, 0))] + [tile] * len(base) + [ANY] * len(bufs),
        out_specs=tile,
        scratch_shapes=[pltpu.VMEM((deep, width), BF16), pltpu.VMEM((8, deep), F32),
                        pltpu.SemaphoreType.DMA((len(bufs),))],
        cost_estimate=pl.CostEstimate(flops=4 * tok * deep * width, bytes_accessed=2 * 10**7, transcendentals=0),
        compiler_params=pltpu.CompilerParams(vmem_limit_bytes=62 * MIB),
    )(table, meta, *base, *bufs)


def solution(mesh):
    token_spec = P(("dp", "ep"), None)
    expert_spec = P("ep", None, None)

    def local_block(hidden, expert_ids, norm_gain, w_router, w_gate, w_up, w_down):
        tok, _ = hidden.shape
        experts = w_router.shape[1]
        per = w_gate.shape[0]
        group = experts // per
        cap = (5 * tok + 2 * experts - 1) // (2 * experts)

        def swap(x, k):
            return lax.ppermute(x, "ep", [(i, i ^ k) for i in range(group)])

        def after(x, *earlier):
            return lax.optimization_barrier((x, *earlier))[0]

        idst = expert_ids.T
        normed, queue, meta, table, *far0 = route(
            hidden, idst, norm_gain, w_router.T, group, cap)
        got0 = [swap(far0[0], 2), swap(far0[1], 3)]
        kept = table[:, :experts]
        even, odd = kept[:, 0::2], kept[:, 1::2]
        spill_out = jnp.any(up_to(even, BLK) + odd > 2 * cap - TAIL)
        spill_back = jnp.any(up_to(odd, BLK) + jnp.maximum(even - (cap - TAIL), 0) > cap)

        def swap_if(spill, xs):
            return lax.cond(spill, lambda a, b: (swap(a, 2), swap(b, 3)), lambda a, b: (a, b), *xs)

        own0, sib0, b2, c2, b3, c3, own1, sib1 = pack(
            [(0, (0,), 0), (1, (0,), 0), (2, (0, 1), cap), (3, (0, 1), cap), (0, (1,), 0), (1, (1,), 0)],
            [cap, cap, cap - TAIL, TAIL, cap - TAIL, TAIL, cap, cap], normed, queue, group, cap)
        sib0, sib1 = swap(sib0, 1), swap(sib1, 1)
        got1 = [swap(b2, 2), swap(b3, 3)]

        def run(mode, i, k, xs, rows, *earlier):
            return ffn(mode, after(table, *earlier), xs, rows, w_gate, w_up, w_down, i, k, cap)

        o_own0, o_sib0 = run("near", 0, 0, [own0, sib0], [cap] * 2)
        o_far0 = run("far0", 0, 2, got0, [cap - TAIL] * 2 + [TAIL] * 2, o_own0)
        extra = swap_if(spill_out, after((c2, c3), *got1))
        back0 = [swap(after(o_far0[j], *got1), 2 + j) for j in range(2)]
        o_far1 = run("far1", 1, 2, [*got0, *got1, *extra, *o_far0[2:]], [cap] * 2 + [TAIL] * 2)
        back1 = [swap(o_far1[0], 2), swap(o_far1[1], 3)]
        back2 = swap_if(spill_back, o_far1[2:])
        o_own1, o_sib1 = run("near", 1, 0, [own1, sib1], [cap] * 2, *back2)
        sib_back0 = swap(after(o_sib0, o_far1[0]), 1)
        sib_back1 = swap(o_sib1, 1)
        near = merge(table, meta, [o_own0, o_own1, sib_back0, sib_back1], group, per, cap)
        bufs = []
        for j in range(2):
            bufs += [back0[j], back1[j], back2[j]]
        return merge(table, meta, bufs, group, per, cap, (near, hidden))

    return jax.shard_map(local_block, mesh=mesh,
                         in_specs=(token_spec, token_spec, P(None), P(None, None), expert_spec, expert_spec, expert_spec),
                         out_specs=token_spec, check_vma=False)
```

profile of v0, /device:TPU:5, one launch (start us, length us, event | category | flops | bytes accessed | tf_op | source)
XLA Modules:
  0.0 414.4 jit_solution(4591179349844841145)
XLA Ops:
  0.0 10.2 %shard_map.73 = (bf16[1024,2048]{1,0:T(8,128)(2,1)}, s32[8,1024]{1,0:T(8,128)}, f32[1024,8]{1,0:T(8,128)}, s32[8,128]{1,0:T(8,128)}, bf16[320,2048]{1,0:T(8,128)(2,1)}, /*index=5*/bf16[320,2048]{1,0:T(8,128)(2,1)}) custom-call(bf16[1024,2048]{1,0:T(8,128)(2,1)} %refs_1_.1, s32[2,1024]{1,0:T(2,128)} %bitcast.6, bf16[2048]{0:T(1024)(128)(2,1)} %gain.1, ...), custom_call_target="tpu_custom_call" | custom-call | flops 10000000000 | bytes 20000000 | tf_op jit(solution)/shard_map/pallas_call | solution.py:136
  10.2 25.5 %shard_map.74 = (bf16[320,2048]{1,0:T(8,128)(2,1)}, bf16[320,2048]{1,0:T(8,128)(2,1)}, bf16[272,2048]{1,0:T(8,128)(2,1)}, bf16[48,2048]{1,0:T(8,128)(2,1)S(1)}, ...) custom-call(bf16[1024,2048]{1,0:T(8,128)(2,1)} %get-tuple-element.64, ...), custom_call_target="tpu_custom_call" | custom-call | flops 8999999488 | bytes 20000000 | tf_op jit(solution)/shard_map/pallas_call | solution.py:160
  35.7 0.7 collective-permute-start.4
  36.4 1.2 collective-permute-start.7
  37.6 0.5 collective-permute-start.8
  38.1 1.2 collective-permute-start.5
  39.3 0.6 collective-permute-start.6
  40.0 0.1 slice.10
  40.1 0.7 fusion.10
  41.4 21.5 %collective-permute-done.7.refs_2_ = bf16[272,2048]{1,0:T(8,128)(2,1)} collective-permute-done((bf16[272,2048]{1,0:T(8,128)(2,1)}, bf16[272,2048]{1,0:T(8,128)(2,1)}, u32[]{:S(2)}, u32[]{:S(2)}) %collective-permute-start.7) | collective-permute-done | bytes 1114144 | tf_op jit(solution)/shard_map/ppermute | solution.py:373
  62.8 24.6 %collective-permute-done.8.refs_3_ = bf16[272,2048]{1,0:T(8,128)(2,1)} collective-permute-done((bf16[272,2048]{1,0:T(8,128)(2,1)}, bf16[272,2048]{1,0:T(8,128)(2,1)}, u32[]{:S(2)}, u32[]{:S(2)}) %collective-permute-start.8) | collective-permute-done | bytes 1114144 | tf_op jit(solution)/shard_map/ppermute | solution.py:373
  88.1 42.7 %shard_map.75 = (bf16[320,2048]{1,0:T(8,128)(2,1)}, bf16[320,2048]{1,0:T(8,128)(2,1)}) custom-call(s32[8,128]{1,0:T(8,128)} %get-tuple-element.86.table, bf16[320,2048]{1,0:T(8,128)(2,1)} %get-tuple-element.66.refs_0_, bf16[320,2048]{1,0:T(8,128)(2,1)} %collective-permute-done.4.refs_1_, bf16[2,2048,5632]{2,1,0:T(8,128)(2,1)} %refs_2_.5, ...), custom_call_target="tpu_custom_call" | custom-call | flops 37371248640 | bytes 69206016 | tf_op jit(solution)/shard_map/pallas_call | solution.py:285
  130.8 12.2 %collective-permute-done.6.refs_1_ = bf16[320,2048]{1,0:T(8,128)(2,1)} collective-permute-done((bf16[320,2048]{1,0:T(8,128)(2,1)}, bf16[320,2048]{1,0:T(8,128)(2,1)}, u32[]{:S(2)}, u32[]{:S(2)}) %collective-permute-start.6) | collective-permute-done | bytes 1310752 | tf_op jit(solution)/shard_map/ppermute | solution.py:373
  143.1 40.9 %shard_map.76 = (bf16[272,2048]{1,0:T(8,128)(2,1)}, bf16[272,2048]{1,0:T(8,128)(2,1)}, bf16[48,2048]{1,0:T(8,128)(2,1)}, bf16[48,2048]{1,0:T(8,128)(2,1)}) custom-call(s32[8,128]{1,0:T(8,128)} %get-tuple-element.86.table, bf16[320,2048]{1,0:T(8,128)(2,1)} %copy-done, bf16[320,2048]{1,0:T(8,128)(2,1)} %collective-permute-done.6.refs_1_, ...), custom_call_target="tpu_custom_call" | custom-call | flops 37371248640 | bytes 69206016 | tf_op jit(solution)/shard_map/pallas_call | solution.py:285
  184.0 45.8 %shard_map.77 = (bf16[320,2048]{1,0:T(8,128)(2,1)}, bf16[320,2048]{1,0:T(8,128)(2,1)}, bf16[48,2048]{1,0:T(8,128)(2,1)S(1)}, bf16[48,2048]{1,0:T(8,128)(2,1)S(1)}) custom-call(s32[8,128]{1,0:T(8,128)} %get-tuple-element.86.table, bf16[320,2048]{1,0:T(8,128)(2,1)} %copy-done, bf16[320,2048]{1,0:T(8,128)(2,1)} %collective-permute-done.6.refs_1_, ...), custom_call_target="tpu_custom_call" | custom-call | flops 37371248640 | bytes 69206016 | tf_op jit(solution)/shard_map/pallas_call | solution.py:285
  229.8 11.3 %collective-permute-start.10 = (bf16[320,2048]{1,0:T(8,128)(2,1)}, bf16[320,2048]{1,0:T(8,128)(2,1)}, u32[]{:S(2)}, u32[]{:S(2)}) collective-permute-start(bf16[320,2048]{1,0:T(8,128)(2,1)} %get-tuple-element.92), channel_id=1, source_target_pairs={{0,1},{1,0},{2,3},{3,2},{4,5},{5,4},{6,7},{7,6}} | collective-permute-start | bytes 3932168 | tf_op jit(solution)/shard_map/ppermute | solution.py:373
  241.1 47.8 %shard_map.78 = (bf16[320,2048]{1,0:T(8,128)(2,1)}, bf16[320,2048]{1,0:T(8,128)(2,1)}) custom-call(s32[8,128]{1,0:T(8,128)} %get-tuple-element.86.table, bf16[320,2048]{1,0:T(8,128)(2,1)} %get-tuple-element.87.refs_0_, bf16[320,2048]{1,0:T(8,128)(2,1)} %collective-permute-done.9.refs_1_, bf16[2,2048,5632]{2,1,0:T(8,128)(2,1)} %refs_2_.5, ...), custom_call_target="tpu_custom_call" | custom-call | flops 37371248640 | bytes 69206016 | tf_op jit(solution)/shard_map/pallas_call | solution.py:285
  289.0 1.8 collective-permute-start.13
  290.8 0.3 collective-permute-start.14
  291.0 1.4 collective-permute-start.12
  292.4 16.6 %shard_map.79.refs_0_ = f32[1024,2048]{1,0:T(8,128)} custom-call(s32[8,128]{1,0:T(8,128)} %get-tuple-element.86.table, f32[1024,8]{1,0:T(8,128)} %get-tuple-element.63.meta, bf16[320,2048]{1,0:T(8,128)(2,1)} %get-tuple-element.68.refs_0_, bf16[320,2048]{1,0:T(8,128)(2,1)} %get-tuple-element.89.refs_1_, bf16[320,2048]{1,0:T(8,128)(2,1)} %collective-permute-done.10.refs_2_, ...), custom_call_target="tpu_custom_call" | custom-call | flops 10737418240 | bytes 20000000 | tf_op jit(solution)/shard_map/pallas_call | solution.py:348
  309.0 63.3 %collective-permute-done.14.refs_5_ = bf16[272,2048]{1,0:T(8,128)(2,1)} collective-permute-done((bf16[272,2048]{1,0:T(8,128)(2,1)}, bf16[272,2048]{1,0:T(8,128)(2,1)}, u32[]{:S(2)}, u32[]{:S(2)}) %collective-permute-start.14) | collective-permute-done | bytes 1114144 | tf_op jit(solution)/shard_map/ppermute | solution.py:373
  372.3 23.7 %collective-permute-done.12.refs_2_ = bf16[272,2048]{1,0:T(8,128)(2,1)} collective-permute-done((bf16[272,2048]{1,0:T(8,128)(2,1)}, bf16[272,2048]{1,0:T(8,128)(2,1)}, u32[]{:S(2)}, u32[]{:S(2)}) %collective-permute-start.12) | collective-permute-done | bytes 1114144 | tf_op jit(solution)/shard_map/ppermute | solution.py:373
  396.0 17.9 %shard_map.80 = bf16[1024,2048]{1,0:T(8,128)(2,1)} custom-call(s32[8,128]{1,0:T(8,128)} %get-tuple-element.86.table, f32[1024,8]{1,0:T(8,128)} %get-tuple-element.63.meta, f32[1024,2048]{1,0:T(8,128)} %shard_map.79.refs_0_, bf16[1024,2048]{1,0:T(8,128)(2,1)} %refs_1_.1, bf16[272,2048]{1,0:T(8,128)(2,1)} %collective-permute-done.12.refs_2_, ...), custom_call_target="tpu_custom_call" | custom-call | flops 10737418240 | bytes 20000000 | tf_op jit(solution)/shard_map/pallas_call | solution.py:348
  (19 shorter events, 0.2 us)
Async XLA Ops:
  10.2 29.7 %copy-start.1 = (s32[8,128]{1,0:T(8,128)S(1)}, s32[8,128]{1,0:T(8,128)}, u32[]{:S(2)}) copy-start(s32[8,128]{1,0:T(8,128)} %get-tuple-element.86.table) | copy-start | bytes 12292
  35.7 52.4 %collective-permute-start.4 = (bf16[320,2048]{1,0:T(8,128)(2,1)}, bf16[320,2048]{1,0:T(8,128)(2,1)}, u32[]{:S(2)}, u32[]{:S(2)}) collective-permute-start(bf16[320,2048]{1,0:T(8,128)(2,1)} %get-tuple-element.67), channel_id=1, source_target_pairs={{0,1},{1,0},{2,3},{3,2},{4,5},{5,4},{6,7},{7,6}} | collective-permute-start | bytes 3932168 | tf_op jit(solution)/shard_map/ppermute | solution.py:373
  36.4 26.4 %collective-permute-start.7 = (bf16[272,2048]{1,0:T(8,128)(2,1)}, bf16[272,2048]{1,0:T(8,128)(2,1)}, u32[]{:S(2)}, u32[]{:S(2)}) collective-permute-start(bf16[272,2048]{1,0:T(8,128)(2,1)} %get-tuple-element.71), channel_id=1, source_target_pairs={{0,2},{1,3},{2,0},{3,1},{4,6},{5,7},{6,4},{7,5}} | collective-permute-start | bytes 3342344 | tf_op jit(solution)/shard_map/ppermute | solution.py:373
  37.6 49.8 %collective-permute-start.8 = (bf16[272,2048]{1,0:T(8,128)(2,1)}, bf16[272,2048]{1,0:T(8,128)(2,1)}, u32[]{:S(2)}, u32[]{:S(2)}) collective-permute-start(bf16[272,2048]{1,0:T(8,128)(2,1)} %get-tuple-element.72), channel_id=1, source_target_pairs={{0,3},{1,2},{2,1},{3,0},{4,7},{5,6},{6,5},{7,4}} | collective-permute-start | bytes 3342344 | tf_op jit(solution)/shard_map/ppermute | solution.py:373
  38.1 92.7 %collective-permute-start.5 = (bf16[320,2048]{1,0:T(8,128)(2,1)}, bf16[320,2048]{1,0:T(8,128)(2,1)S(1)}, u32[]{:S(2)}, u32[]{:S(2)}) collective-permute-start(bf16[320,2048]{1,0:T(8,128)(2,1)} %get-tuple-element.69), channel_id=1, source_target_pairs={{0,2},{1,3},{2,0},{3,1},{4,6},{5,7},{6,4},{7,5}} | collective-permute-start | bytes 3932168 | tf_op jit(solution)/shard_map/ppermute | solution.py:373
  39.3 103.8 %collective-permute-start.6 = (bf16[320,2048]{1,0:T(8,128)(2,1)}, bf16[320,2048]{1,0:T(8,128)(2,1)}, u32[]{:S(2)}, u32[]{:S(2)}) collective-permute-start(bf16[320,2048]{1,0:T(8,128)(2,1)} %get-tuple-element.70), channel_id=1, source_target_pairs={{0,3},{1,2},{2,1},{3,0},{4,7},{5,6},{6,5},{7,4}} | collective-permute-start | bytes 3932168 | tf_op jit(solution)/shard_map/ppermute | solution.py:373
  87.4 153.7 %collective-permute-start.9 = (bf16[320,2048]{1,0:T(8,128)(2,1)}, bf16[320,2048]{1,0:T(8,128)(2,1)}, u32[]{:S(2)}, u32[]{:S(2)}) collective-permute-start(bf16[320,2048]{1,0:T(8,128)(2,1)} %get-tuple-element.88), channel_id=1, source_target_pairs={{0,1},{1,0},{2,3},{3,2},{4,5},{5,4},{6,7},{7,6}} | collective-permute-start | bytes 3932168 | tf_op jit(solution)/shard_map/ppermute | solution.py:373
  130.8 12.3 %copy-start = (bf16[320,2048]{1,0:T(8,128)(2,1)}, bf16[320,2048]{1,0:T(8,128)(2,1)S(1)}, u32[]{:S(2)}) copy-start(bf16[320,2048]{1,0:T(8,128)(2,1)S(1)} %collective-permute-done.5.refs_0_) | copy-start | bytes 3932164
  229.8 61.3 %collective-permute-start.10 = (bf16[320,2048]{1,0:T(8,128)(2,1)}, bf16[320,2048]{1,0:T(8,128)(2,1)}, u32[]{:S(2)}, u32[]{:S(2)}) collective-permute-start(bf16[320,2048]{1,0:T(8,128)(2,1)} %get-tuple-element.92), channel_id=1, source_target_pairs={{0,1},{1,0},{2,3},{3,2},{4,5},{5,4},{6,7},{7,6}} | collective-permute-start | bytes 3932168 | tf_op jit(solution)/shard_map/ppermute | solution.py:373
  241.1 47.8 %copy-start.2 = (bf16[320,2048]{1,0:T(8,128)(2,1)S(1)}, bf16[320,2048]{1,0:T(8,128)(2,1)}, u32[]{:S(2)}) copy-start(bf16[320,2048]{1,0:T(8,128)(2,1)} %get-tuple-element.91) | copy-start | bytes 3932164
  288.9 3.6 collective-permute-start.11
  288.9 107.1 %collective-permute-start.15 = (bf16[320,2048]{1,0:T(8,128)(2,1)}, bf16[320,2048]{1,0:T(8,128)(2,1)}, u32[]{:S(2)}, u32[]{:S(2)}) collective-permute-start(bf16[320,2048]{1,0:T(8,128)(2,1)} %get-tuple-element.98), channel_id=1, source_target_pairs={{0,3},{1,2},{2,1},{3,0},{4,7},{5,6},{6,5},{7,4}} | collective-permute-start | bytes 3932168 | tf_op jit(solution)/shard_map/ppermute | solution.py:373
  289.0 107.1 %collective-permute-start.13 = (bf16[320,2048]{1,0:T(8,128)(2,1)S(1)}, bf16[320,2048]{1,0:T(8,128)(2,1)}, u32[]{:S(2)}, u32[]{:S(2)}) collective-permute-start(bf16[320,2048]{1,0:T(8,128)(2,1)S(1)} %copy-done.2), channel_id=1, source_target_pairs={{0,2},{1,3},{2,0},{3,1},{4,6},{5,7},{6,4},{7,5}} | collective-permute-start | bytes 3932168 | tf_op jit(solution)/shard_map/ppermute | solution.py:373
  290.8 81.5 %collective-permute-start.14 = (bf16[272,2048]{1,0:T(8,128)(2,1)}, bf16[272,2048]{1,0:T(8,128)(2,1)}, u32[]{:S(2)}, u32[]{:S(2)}) collective-permute-start(bf16[272,2048]{1,0:T(8,128)(2,1)} %get-tuple-element.97), channel_id=1, source_target_pairs={{0,3},{1,2},{2,1},{3,0},{4,7},{5,6},{6,5},{7,4}} | collective-permute-start | bytes 3342344 | tf_op jit(solution)/shard_map/ppermute | solution.py:373
  291.0 105.0 %collective-permute-start.12 = (bf16[272,2048]{1,0:T(8,128)(2,1)}, bf16[272,2048]{1,0:T(8,128)(2,1)}, u32[]{:S(2)}, u32[]{:S(2)}) collective-permute-start(bf16[272,2048]{1,0:T(8,128)(2,1)} %get-tuple-element.95), channel_id=1, source_target_pairs={{0,2},{1,3},{2,0},{3,1},{4,6},{5,7},{6,4},{7,5}} | collective-permute-start | bytes 3342344 | tf_op jit(solution)/shard_map/ppermute | solution.py:373
where the time goes:
time: 421 us; the launch traced here: 414 us
  Pallas kernels  247 us (59%)
  waiting for transfers between devices  145 us (34%)
  starting transfers between devices  19.1 us (5%)
    pallas_call x4, Pallas kernels, ffn(): pl.pallas_call(functools.partial(ffn_kernel, mode, local, wg.shape[0], di...  177 us
    ppermute x12, waiting for transfers between devices, swap(): return lax.ppermute(x, 'ep', [(i, i ^ k) for i in range(group)])  145 us
    pallas_call x2, Pallas kernels, merge(): pl.pallas_call(functools.partial(merge_kernel, group, per, cap, len(bufs)...  34.5 us
    pallas_call x1, Pallas kernels, pack(): pl.pallas_call(functools.partial(pack_kernel, group, queue.shape[0] // gr...  25.5 us
    ppermute x12, starting transfers between devices, swap(): return lax.ppermute(x, 'ep', [(i, i ^ k) for i in range(group)])  19.1 us
    pallas_call x1, Pallas kernels, route(): pl.pallas_call(functools.partial(route_kernel, group, experts // group, c...  10.2 us
  transfers between devices with their start and end apart: 12, of which 5 were waited for; matrix products, arithmetic and copies ran while one was open for 0% of the time, Pallas kernels for 47%

commit v1 on v0

--- a/solution.py
+++ b/solution.py
@@ -387,16 +387,17 @@
         def swap_if(spill, xs):
             return lax.cond(spill, lambda a, b: (swap(a, 2), swap(b, 3)), lambda a, b: (a, b), *xs)
 
-        own0, sib0, b2, c2, b3, c3, own1, sib1 = pack(
-            [(0, (0,), 0), (1, (0,), 0), (2, (0, 1), cap), (3, (0, 1), cap), (0, (1,), 0), (1, (1,), 0)],
-            [cap, cap, cap - TAIL, TAIL, cap - TAIL, TAIL, cap, cap], normed, queue, group, cap)
+        own0, sib0, b2, c2, b3, c3 = pack(
+            [(0, (0,), 0), (1, (0,), 0), (2, (0, 1), cap), (3, (0, 1), cap)],
+            [cap, cap, cap - TAIL, TAIL, cap - TAIL, TAIL], normed, queue, group, cap)
+        own1, sib1 = pack([(0, (1,), 0), (1, (1,), 0)], [cap] * 2, after(normed, own0), queue, group, cap)
         sib0, sib1 = swap(sib0, 1), swap(sib1, 1)
         got1 = [swap(b2, 2), swap(b3, 3)]
 
         def run(mode, i, k, xs, rows, *earlier):
             return ffn(mode, after(table, *earlier), xs, rows, w_gate, w_up, w_down, i, k, cap)
 
-        o_own0, o_sib0 = run("near", 0, 0, [own0, sib0], [cap] * 2)
+        o_own0, o_sib0 = run("near", 0, 0, [own0, sib0], [cap] * 2, own1)
         o_far0 = run("far0", 0, 2, got0, [cap - TAIL] * 2 + [TAIL] * 2, o_own0)
         extra = swap_if(spill_out, after((c2, c3), *got1))
         back0 = [swap(after(o_far0[j], *got1), 2 + j) for j in range(2)]

time: 421 us -> 405 us (0.962)
  Pallas kernels: 247 us -> 237 us
  waiting for transfers between devices: 145 us -> 139 us
    pallas_call x1 -> x2, Pallas kernels: 25.5 us -> 15.7 us  [pack(): pl.pallas_call(functools.partial(pack_kernel, group, queue.shape[0] // gr...]
    ppermute x12, waiting for transfers between devices: 145 us -> 139 us  [swap(): return lax.ppermute(x, 'ep', [(i, i ^ k) for i in range(group)])]
  transfers between devices with their start and end apart: 12 -> 12, of which waited for: 5 -> 5; matrix products, arithmetic and copies ran while one was open for 0% -> 0% of each run, Pallas kernels for 47% -> 50%
where the time goes in v1:
time: 405 us; the launch traced here: 398 us
  Pallas kernels  237 us (59%)
  waiting for transfers between devices  139 us (34%)
  starting transfers between devices  19.1 us (5%)
    pallas_call x4, Pallas kernels, ffn(): pl.pallas_call(functools.partial(ffn_kernel, mode, local, wg.shape[0], di...  177 us
    ppermute x12, waiting for transfers between devices, swap(): return lax.ppermute(x, 'ep', [(i, i ^ k) for i in range(group)])  139 us
    pallas_call x2, Pallas kernels, merge(): pl.pallas_call(functools.partial(merge_kernel, group, per, cap, len(bufs)...  34.4 us
    ppermute x12, starting transfers between devices, swap(): return lax.ppermute(x, 'ep', [(i, i ^ k) for i in range(group)])  19.1 us
    pallas_call x2, Pallas kernels, pack(): pl.pallas_call(functools.partial(pack_kernel, group, queue.shape[0] // gr...  15.7 us
    pallas_call x1, Pallas kernels, route(): pl.pallas_call(functools.partial(route_kernel, group, experts // group, c...  10.3 us
  transfers between devices with their start and end apart: 12, of which 5 were waited for; matrix products, arithmetic and copies ran while one was open for 0% of the time, Pallas kernels for 50%

profile of v1, /device:TPU:5, one launch (start us, length us, event | category | flops | bytes accessed | tf_op | source)
XLA Modules:
  0.0 398.3 jit_solution(16933355909633953612)
XLA Ops:
  0.0 10.3 %shard_map.73 = (bf16[1024,2048]{1,0:T(8,128)(2,1)}, s32[8,1024]{1,0:T(8,128)}, f32[1024,8]{1,0:T(8,128)}, s32[8,128]{1,0:T(8,128)}, bf16[320,2048]{1,0:T(8,128)(2,1)}, /*index=5*/bf16[320,2048]{1,0:T(8,128)(2,1)}) custom-call(bf16[1024,2048]{1,0:T(8,128)(2,1)} %refs_1_.1, s32[2,1024]{1,0:T(2,128)} %bitcast.6, bf16[2048]{0:T(1024)(128)(2,1)} %gain.1, ...), custom_call_target="tpu_custom_call" | custom-call | flops 10000000000 | bytes 20000000 | tf_op jit(solution)/shard_map/pallas_call | solution.py:136
  10.3 9.5 %shard_map.74 = (bf16[320,2048]{1,0:T(8,128)(2,1)}, bf16[320,2048]{1,0:T(8,128)(2,1)}, bf16[272,2048]{1,0:T(8,128)(2,1)}, bf16[48,2048]{1,0:T(8,128)(2,1)S(1)}, ...) custom-call(bf16[1024,2048]{1,0:T(8,128)(2,1)} %get-tuple-element.69.normed, s32[8,1024]{1,0:T(8,128)} %get-tuple-element.67.queue), custom_call_target="tpu_custom_call" | custom-call | flops 8999999488 | bytes 20000000 | tf_op jit(solution)/shard_map/pallas_call | solution.py:160
  19.8 0.7 collective-permute-start.4
  20.5 1.2 collective-permute-start.7
  21.7 0.5 collective-permute-start.8
  22.2 1.2 collective-permute-start.5
  23.4 0.6 collective-permute-start.6
  24.2 0.7 fusion.10
  25.5 6.1 %shard_map.75 = (bf16[320,2048]{1,0:T(8,128)(2,1)}, bf16[320,2048]{1,0:T(8,128)(2,1)}) custom-call(bf16[1024,2048]{1,0:T(8,128)(2,1)} %get-tuple-element.69.normed, s32[8,1024]{1,0:T(8,128)} %get-tuple-element.67.queue), custom_call_target="tpu_custom_call" | custom-call | flops 8999999488 | bytes 20000000 | tf_op jit(solution)/shard_map/pallas_call | solution.py:160
  31.6 15.3 %collective-permute-done.7.refs_2_ = bf16[272,2048]{1,0:T(8,128)(2,1)} collective-permute-done((bf16[272,2048]{1,0:T(8,128)(2,1)}, bf16[272,2048]{1,0:T(8,128)(2,1)}, u32[]{:S(2)}, u32[]{:S(2)}) %collective-permute-start.7) | collective-permute-done | bytes 1114144 | tf_op jit(solution)/shard_map/ppermute | solution.py:373
  46.9 24.6 %collective-permute-done.8.refs_3_ = bf16[272,2048]{1,0:T(8,128)(2,1)} collective-permute-done((bf16[272,2048]{1,0:T(8,128)(2,1)}, bf16[272,2048]{1,0:T(8,128)(2,1)}, u32[]{:S(2)}, u32[]{:S(2)}) %collective-permute-start.8) | collective-permute-done | bytes 1114144 | tf_op jit(solution)/shard_map/ppermute | solution.py:373
  72.1 42.7 %shard_map.76 = (bf16[320,2048]{1,0:T(8,128)(2,1)}, bf16[320,2048]{1,0:T(8,128)(2,1)}) custom-call(s32[8,128]{1,0:T(8,128)} %get-tuple-element.91.table, bf16[320,2048]{1,0:T(8,128)(2,1)} %get-tuple-element.68.refs_0_, bf16[320,2048]{1,0:T(8,128)(2,1)} %collective-permute-done.4.refs_1_, bf16[2,2048,5632]{2,1,0:T(8,128)(2,1)} %refs_2_.5, ...), custom_call_target="tpu_custom_call" | custom-call | flops 37371248640 | bytes 69206016 | tf_op jit(solution)/shard_map/pallas_call | solution.py:285
  114.8 12.4 %collective-permute-done.6.refs_1_ = bf16[320,2048]{1,0:T(8,128)(2,1)} collective-permute-done((bf16[320,2048]{1,0:T(8,128)(2,1)}, bf16[320,2048]{1,0:T(8,128)(2,1)}, u32[]{:S(2)}, u32[]{:S(2)}) %collective-permute-start.6) | collective-permute-done | bytes 1310752 | tf_op jit(solution)/shard_map/ppermute | solution.py:373
  127.2 40.8 %shard_map.77 = (bf16[272,2048]{1,0:T(8,128)(2,1)}, bf16[272,2048]{1,0:T(8,128)(2,1)}, bf16[48,2048]{1,0:T(8,128)(2,1)}, bf16[48,2048]{1,0:T(8,128)(2,1)}) custom-call(s32[8,128]{1,0:T(8,128)} %get-tuple-element.91.table, bf16[320,2048]{1,0:T(8,128)(2,1)} %copy-done, bf16[320,2048]{1,0:T(8,128)(2,1)} %collective-permute-done.6.refs_1_, ...), custom_call_target="tpu_custom_call" | custom-call | flops 37371248640 | bytes 69206016 | tf_op jit(solution)/shard_map/pallas_call | solution.py:285
  168.0 45.8 %shard_map.78 = (bf16[320,2048]{1,0:T(8,128)(2,1)}, bf16[320,2048]{1,0:T(8,128)(2,1)}, bf16[48,2048]{1,0:T(8,128)(2,1)S(1)}, bf16[48,2048]{1,0:T(8,128)(2,1)S(1)}) custom-call(s32[8,128]{1,0:T(8,128)} %get-tuple-element.91.table, bf16[320,2048]{1,0:T(8,128)(2,1)} %copy-done, bf16[320,2048]{1,0:T(8,128)(2,1)} %collective-permute-done.6.refs_1_, ...), custom_call_target="tpu_custom_call" | custom-call | flops 37371248640 | bytes 69206016 | tf_op jit(solution)/shard_map/pallas_call | solution.py:285
  213.9 11.3 %collective-permute-start.10 = (bf16[320,2048]{1,0:T(8,128)(2,1)}, bf16[320,2048]{1,0:T(8,128)(2,1)}, u32[]{:S(2)}, u32[]{:S(2)}) collective-permute-start(bf16[320,2048]{1,0:T(8,128)(2,1)} %get-tuple-element.96), channel_id=1, source_target_pairs={{0,1},{1,0},{2,3},{3,2},{4,5},{5,4},{6,7},{7,6}} | collective-permute-start | bytes 3932168 | tf_op jit(solution)/shard_map/ppermute | solution.py:373
  225.2 47.6 %shard_map.79 = (bf16[320,2048]{1,0:T(8,128)(2,1)}, bf16[320,2048]{1,0:T(8,128)(2,1)}) custom-call(s32[8,128]{1,0:T(8,128)} %get-tuple-element.91.table, bf16[320,2048]{1,0:T(8,128)(2,1)} %get-tuple-element.70.refs_0_, bf16[320,2048]{1,0:T(8,128)(2,1)} %collective-permute-done.9.refs_1_, bf16[2,2048,5632]{2,1,0:T(8,128)(2,1)} %refs_2_.5, ...), custom_call_target="tpu_custom_call" | custom-call | flops 37371248640 | bytes 69206016 | tf_op jit(solution)/shard_map/pallas_call | solution.py:285
  272.9 1.8 collective-permute-start.13
  274.7 0.3 collective-permute-start.14
  275.0 1.4 collective-permute-start.12
  276.4 16.6 %shard_map.80.refs_0_ = f32[1024,2048]{1,0:T(8,128)} custom-call(s32[8,128]{1,0:T(8,128)} %get-tuple-element.91.table, f32[1024,8]{1,0:T(8,128)} %get-tuple-element.65.meta, bf16[320,2048]{1,0:T(8,128)(2,1)} %get-tuple-element.73.refs_0_, bf16[320,2048]{1,0:T(8,128)(2,1)} %get-tuple-element.93.refs_1_, bf16[320,2048]{1,0:T(8,128)(2,1)} %collective-permute-done.10.refs_2_, ...), custom_call_target="tpu_custom_call" | custom-call | flops 10737418240 | bytes 20000000 | tf_op jit(solution)/shard_map/pallas_call | solution.py:348
  293.0 63.3 %collective-permute-done.14.refs_5_ = bf16[272,2048]{1,0:T(8,128)(2,1)} collective-permute-done((bf16[272,2048]{1,0:T(8,128)(2,1)}, bf16[272,2048]{1,0:T(8,128)(2,1)}, u32[]{:S(2)}, u32[]{:S(2)}) %collective-permute-start.14) | collective-permute-done | bytes 1114144 | tf_op jit(solution)/shard_map/ppermute | solution.py:373
  356.3 23.7 %collective-permute-done.12.refs_2_ = bf16[272,2048]{1,0:T(8,128)(2,1)} collective-permute-done((bf16[272,2048]{1,0:T(8,128)(2,1)}, bf16[272,2048]{1,0:T(8,128)(2,1)}, u32[]{:S(2)}, u32[]{:S(2)}) %collective-permute-start.12) | collective-permute-done | bytes 1114144 | tf_op jit(solution)/shard_map/ppermute | solution.py:373
  380.0 17.8 %shard_map.81 = bf16[1024,2048]{1,0:T(8,128)(2,1)} custom-call(s32[8,128]{1,0:T(8,128)} %get-tuple-element.91.table, f32[1024,8]{1,0:T(8,128)} %get-tuple-element.65.meta, f32[1024,2048]{1,0:T(8,128)} %shard_map.80.refs_0_, bf16[1024,2048]{1,0:T(8,128)(2,1)} %refs_1_.1, bf16[272,2048]{1,0:T(8,128)(2,1)} %collective-permute-done.12.refs_2_, ...), custom_call_target="tpu_custom_call" | custom-call | flops 10737418240 | bytes 20000000 | tf_op jit(solution)/shard_map/pallas_call | solution.py:348
  (20 shorter events, 0.3 us)
Async XLA Ops:
  10.3 13.8 %copy-start.1 = (s32[8,128]{1,0:T(8,128)S(1)}, s32[8,128]{1,0:T(8,128)}, u32[]{:S(2)}) copy-start(s32[8,128]{1,0:T(8,128)} %get-tuple-element.91.table) | copy-start | bytes 12292
  19.8 52.3 %collective-permute-start.4 = (bf16[320,2048]{1,0:T(8,128)(2,1)}, bf16[320,2048]{1,0:T(8,128)(2,1)}, u32[]{:S(2)}, u32[]{:S(2)}) collective-permute-start(bf16[320,2048]{1,0:T(8,128)(2,1)} %get-tuple-element.72), channel_id=1, source_target_pairs={{0,1},{1,0},{2,3},{3,2},{4,5},{5,4},{6,7},{7,6}} | collective-permute-start | bytes 3932168 | tf_op jit(solution)/shard_map/ppermute | solution.py:373
  20.5 26.4 %collective-permute-start.7 = (bf16[272,2048]{1,0:T(8,128)(2,1)}, bf16[272,2048]{1,0:T(8,128)(2,1)}, u32[]{:S(2)}, u32[]{:S(2)}) collective-permute-start(bf16[272,2048]{1,0:T(8,128)(2,1)} %get-tuple-element.76), channel_id=1, source_target_pairs={{0,2},{1,3},{2,0},{3,1},{4,6},{5,7},{6,4},{7,5}} | collective-permute-start | bytes 3342344 | tf_op jit(solution)/shard_map/ppermute | solution.py:373
  21.7 49.8 %collective-permute-start.8 = (bf16[272,2048]{1,0:T(8,128)(2,1)}, bf16[272,2048]{1,0:T(8,128)(2,1)}, u32[]{:S(2)}, u32[]{:S(2)}) collective-permute-start(bf16[272,2048]{1,0:T(8,128)(2,1)} %get-tuple-element.77), channel_id=1, source_target_pairs={{0,3},{1,2},{2,1},{3,0},{4,7},{5,6},{6,5},{7,4}} | collective-permute-start | bytes 3342344 | tf_op jit(solution)/shard_map/ppermute | solution.py:373
  22.2 92.6 %collective-permute-start.5 = (bf16[320,2048]{1,0:T(8,128)(2,1)}, bf16[320,2048]{1,0:T(8,128)(2,1)S(1)}, u32[]{:S(2)}, u32[]{:S(2)}) collective-permute-start(bf16[320,2048]{1,0:T(8,128)(2,1)} %get-tuple-element.74), channel_id=1, source_target_pairs={{0,2},{1,3},{2,0},{3,1},{4,6},{5,7},{6,4},{7,5}} | collective-permute-start | bytes 3932168 | tf_op jit(solution)/shard_map/ppermute | solution.py:373
  23.4 103.8 %collective-permute-start.6 = (bf16[320,2048]{1,0:T(8,128)(2,1)}, bf16[320,2048]{1,0:T(8,128)(2,1)}, u32[]{:S(2)}, u32[]{:S(2)}) collective-permute-start(bf16[320,2048]{1,0:T(8,128)(2,1)} %get-tuple-element.75), channel_id=1, source_target_pairs={{0,3},{1,2},{2,1},{3,0},{4,7},{5,6},{6,5},{7,4}} | collective-permute-start | bytes 3932168 | tf_op jit(solution)/shard_map/ppermute | solution.py:373
  71.5 153.7 %collective-permute-start.9 = (bf16[320,2048]{1,0:T(8,128)(2,1)}, bf16[320,2048]{1,0:T(8,128)(2,1)}, u32[]{:S(2)}, u32[]{:S(2)}) collective-permute-start(bf16[320,2048]{1,0:T(8,128)(2,1)} %get-tuple-element.92), channel_id=1, source_target_pairs={{0,1},{1,0},{2,3},{3,2},{4,5},{5,4},{6,7},{7,6}} | collective-permute-start | bytes 3932168 | tf_op jit(solution)/shard_map/ppermute | solution.py:373
  114.8 12.4 %copy-start = (bf16[320,2048]{1,0:T(8,128)(2,1)}, bf16[320,2048]{1,0:T(8,128)(2,1)S(1)}, u32[]{:S(2)}) copy-start(bf16[320,2048]{1,0:T(8,128)(2,1)S(1)} %collective-permute-done.5.refs_0_) | copy-start | bytes 3932164
  213.8 59.1 %copy-start.2 = (bf16[320,2048]{1,0:T(8,128)(2,1)S(1)}, bf16[320,2048]{1,0:T(8,128)(2,1)}, u32[]{:S(2)}) copy-start(bf16[320,2048]{1,0:T(8,128)(2,1)} %get-tuple-element.95) | copy-start | bytes 3932164
  213.9 61.2 %collective-permute-start.10 = (bf16[320,2048]{1,0:T(8,128)(2,1)}, bf16[320,2048]{1,0:T(8,128)(2,1)}, u32[]{:S(2)}, u32[]{:S(2)}) collective-permute-start(bf16[320,2048]{1,0:T(8,128)(2,1)} %get-tuple-element.96), channel_id=1, source_target_pairs={{0,1},{1,0},{2,3},{3,2},{4,5},{5,4},{6,7},{7,6}} | collective-permute-start | bytes 3932168 | tf_op jit(solution)/shard_map/ppermute | solution.py:373
  272.8 3.6 collective-permute-start.11
  272.9 107.1 %collective-permute-start.15 = (bf16[320,2048]{1,0:T(8,128)(2,1)}, bf16[320,2048]{1,0:T(8,128)(2,1)}, u32[]{:S(2)}, u32[]{:S(2)}) collective-permute-start(bf16[320,2048]{1,0:T(8,128)(2,1)} %get-tuple-element.102), channel_id=1, source_target_pairs={{0,3},{1,2},{2,1},{3,0},{4,7},{5,6},{6,5},{7,4}} | collective-permute-start | bytes 3932168 | tf_op jit(solution)/shard_map/ppermute | solution.py:373
  272.9 107.1 %collective-permute-start.13 = (bf16[320,2048]{1,0:T(8,128)(2,1)S(1)}, bf16[320,2048]{1,0:T(8,128)(2,1)}, u32[]{:S(2)}, u32[]{:S(2)}) collective-permute-start(bf16[320,2048]{1,0:T(8,128)(2,1)S(1)} %copy-done.2), channel_id=1, source_target_pairs={{0,2},{1,3},{2,0},{3,1},{4,6},{5,7},{6,4},{7,5}} | collective-permute-start | bytes 3932168 | tf_op jit(solution)/shard_map/ppermute | solution.py:373
  274.7 81.5 %collective-permute-start.14 = (bf16[272,2048]{1,0:T(8,128)(2,1)}, bf16[272,2048]{1,0:T(8,128)(2,1)}, u32[]{:S(2)}, u32[]{:S(2)}) collective-permute-start(bf16[272,2048]{1,0:T(8,128)(2,1)} %get-tuple-element.101), channel_id=1, source_target_pairs={{0,3},{1,2},{2,1},{3,0},{4,7},{5,6},{6,5},{7,4}} | collective-permute-start | bytes 3342344 | tf_op jit(solution)/shard_map/ppermute | solution.py:373
  275.0 105.0 %collective-permute-start.12 = (bf16[272,2048]{1,0:T(8,128)(2,1)}, bf16[272,2048]{1,0:T(8,128)(2,1)}, u32[]{:S(2)}, u32[]{:S(2)}) collective-permute-start(bf16[272,2048]{1,0:T(8,128)(2,1)} %get-tuple-element.99), channel_id=1, source_target_pairs={{0,2},{1,3},{2,0},{3,1},{4,6},{5,7},{6,4},{7,5}} | collective-permute-start | bytes 3342344 | tf_op jit(solution)/shard_map/ppermute | solution.py:373
